TPU v7x, 32 devices: a whole 2x2x4 slice. The times are simulated.
32 devices in a mesh: grp: 2 (over x), pq: 16 (over z, y, core).
Axes of the slice: x: 2, y: 2, z: 4, core: 2. Of those that a mesh axis runs over, the one named last changes fastest.
Arguments:
- pair_blocks: bfloat16 [4, 288, 128, 128], P('grp', 'pq'), may hold values from -6 to 6
- block_list: int32 [4, 288], P('grp', 'pq'), may hold values from 0 to 2047, as said below
- block_count: int32 [4, 16], P('grp', 'pq'), may hold values from 1 to 18, as said below
- coef: bfloat16 [4096, 512], P('pq', 'grp'), may hold values from -0.09375 to 0.09375
Outputs:
- transformed: float32 [8, 512, 512], P('grp', 'pq')
Inputs may be any that keep to these rules, and one draw needn't show every extreme that they name: `block_list`: within one row the ids are distinct, each in 0 to 2 * 32^2 - 1. `block_count`: in every row some device has exactly 18 live slots.
All inputs are finite; a program needn't handle non-finite values.
Results may differ from a plain program's by a relative error of at most 0.0042.
Values may be sent and summed in bfloat16 or wider, within the bound.
A program may use at most 64 MiB of HBM per device.

v0:
```python
import jax
import jax.numpy as jnp
from jax import lax
from jax.sharding import PartitionSpec as P

KL_PANEL = 2


def partner(value, axis, distance):
    mask = 2**distance
    pairs = [(source, source ^ mask) for source in range(lax.axis_size(axis))]
    return lax.ppermute(value, axis, pairs)


def block_term(block, ident, coef_full, tile, nblk):
    per_kl = nblk * nblk
    which = ident // per_kl
    row_blk = ident // nblk % nblk
    col_blk = ident % nblk
    col_coef = lax.dynamic_slice_in_dim(coef_full, col_blk * tile, tile, 0)
    row_coef = lax.dynamic_slice_in_dim(coef_full, row_blk * tile, tile, 0)
    half = jnp.dot(block, col_coef, preferred_element_type=jnp.float32).astype(jnp.bfloat16)
    term = lax.dot_general(
        row_coef, half, (((0,), (0,)), ((), ())), preferred_element_type=jnp.float32
    )
    return (which, term)


def add_term(total, which, term):
    current = lax.dynamic_index_in_dim(total, which, 0, keepdims=False)
    return lax.dynamic_update_index_in_dim(total, current + term, which, 0)


def body(pair_blocks, block_list, block_count, coef):
    coef_rows = lax.all_gather(coef, "pq", axis=0, tiled=True)
    coef_full = lax.all_gather(coef_rows, "grp", axis=1, tiled=True)
    panels = pair_blocks.shape[0]
    tile = pair_blocks.shape[2]
    nblk = coef_full.shape[0] // tile
    width = coef_full.shape[1]
    empty = jnp.zeros((KL_PANEL, width, width), jnp.float32)
    size_pq = lax.axis_size("pq")
    bit = size_pq.bit_length() - 2
    other_blocks, other_list, other_count = partner(
        (pair_blocks, block_list, block_count), "pq", bit
    )
    upper = lax.axis_index("pq") // (size_pq // 2) % 2
    stacked_blocks = jnp.stack([pair_blocks, other_blocks])
    stacked_list = jnp.stack([block_list, other_list])
    pieces = []
    for panel in range(panels):
        own_count = block_count[panel, 0]
        far_count = other_count[panel, 0]
        first_count = jnp.where(upper == 1, far_count, own_count)
        combined = own_count + far_count
        middle = (combined + 1) // 2
        lower_bound = jnp.where(upper == 1, middle, 0)
        upper_bound = jnp.where(upper == 1, combined, middle)

        def step(slot, total):
            source = jnp.where(slot < first_count, upper, 1 - upper)
            place = jnp.where(slot < first_count, slot, slot - first_count)
            block = stacked_blocks[source, panel, place]
            ident = stacked_list[source, panel, place]
            which, term = block_term(block, ident, coef_full, tile, nblk)
            return add_term(total, which, term)

        totals = lax.fori_loop(lower_bound, upper_bound, step, empty)
        pieces.append(totals)
    joined = jnp.concatenate(pieces, 0)
    return lax.psum_scatter(joined, "pq", scatter_dimension=1, tiled=True)


def solution(mesh):
    in_specs = (P("grp", "pq", None, None), P("grp", "pq"), P("grp", "pq"), P("pq", "grp"))
    out_specs = P("grp", "pq", None)
    return jax.shard_map(body, mesh=mesh, in_specs=in_specs, out_specs=out_specs, check_vma=False)
```

profile of v0, /device:TPU:0, one launch (start us, length us, event | category | flops | bytes accessed | tf_op | source)
XLA Modules:
  0.0 345.6 jit_solution(15442970876502260729)
XLA Ops:
  6.5 0.7 all-gather.3.cloned.1.call-update
  7.3 46.4 %all-gather.3.cloned.1.call-done = bf16[4096,256]{1,0:T(8,128)(2,1)} async-done(((bf16[256,256]{1,0:T(8,128)(2,1)}), bf16[4096,256]{1,0:T(8,128)(2,1)}) %all-gather.3.cloned.1.call-update) | async-done | bytes 2097168 | tf_op jit(solution)/shard_map/all_gather | solution.py:35
  53.8 0.7 collective-permute-start.2
  54.5 2.3 collective-permute-start
  56.8 0.6 collective-permute-start.1
  57.4 1.4 fusion.25
  58.8 49.5 %collective-permute-done = s32[2,1]{0,1:T(1,128)S(1)} collective-permute-done((s32[2,1]{0,1:T(1,128)}, s32[2,1]{0,1:T(1,128)S(1)}, u32[]{:S(2)}, u32[]{:S(2)}) %collective-permute-start) | collective-permute-done | bytes 40 | tf_op jit(solution)/shard_map/ppermute | solution.py:12
  108.3 0.6 fusion.24
  113.7 1.7 pad_maximum_fusion.1
  115.4 1.7 broadcast_in_dim.18.clone
  117.0 90.4 %while.27 = (s32[]{:T(128)}, f32[2,512,512]{2,1,0:T(8,128)}, s32[]{:T(128)}, s32[]{:T(128)}, s32[]{:T(128)}, /*index=5*/s32[]{:T(128)}, s32[2,2,18]{2,1,0:T(2,12...) while((s32[]{:T(128)}, f32[2,512,512]{2,1,0:T(8,128)}, ...), condition=%wide.region_3.4_spmd, body=%wide.region_2.3_spmd.sunk | while | flops 84213824 | bytes 4490093 | solution.py:68
  120.2 1.3 constant_dynamic-slice_fusion.11
  121.5 2.4 fusion.41
  123.9 0.6 constant_dynamic-slice_fusion.10
  127.1 1.3 constant_dynamic-slice_fusion.11
  128.4 2.5 fusion.41
  131.0 0.6 constant_dynamic-slice_fusion.10
  134.2 1.3 constant_dynamic-slice_fusion.11
  135.5 2.5 fusion.41
  141.2 1.3 constant_dynamic-slice_fusion.11
  142.5 2.5 fusion.41
  148.2 1.3 constant_dynamic-slice_fusion.11
  149.5 2.4 fusion.41
  151.9 0.6 constant_dynamic-slice_fusion.10
  155.1 1.3 constant_dynamic-slice_fusion.11
  156.4 2.5 fusion.41
  162.1 1.3 constant_dynamic-slice_fusion.11
  163.4 2.4 fusion.41
  165.8 0.6 constant_dynamic-slice_fusion.10
  169.0 1.3 constant_dynamic-slice_fusion.11
  170.3 2.4 fusion.41
  175.9 1.3 constant_dynamic-slice_fusion.11
  177.2 2.4 fusion.41
  182.8 1.3 constant_dynamic-slice_fusion.11
  184.1 2.5 fusion.41
  189.8 1.3 constant_dynamic-slice_fusion.11
  191.1 2.4 fusion.41
  196.7 1.3 constant_dynamic-slice_fusion.11
  198.0 2.5 fusion.41
  203.8 1.3 constant_dynamic-slice_fusion.11
  205.1 2.4 fusion.41
  207.7 47.8 %while.26 = (s32[]{:T(128)}, f32[2,512,512]{2,1,0:T(8,128)S(1)}, s32[]{:T(128)}, s32[]{:T(128)}, s32[]{:T(128)}, /*index=5*/s32[]{:T(128)}, s32[2,2,18]{2,1,0:T(...) while((s32[]{:T(128)}, f32[2,512,512]{2,1,0:T(8,128)S(1)}, ...), condition=%wide.region_1.2_spmd, body=%wide.region_0.1_spmd.sunk | while | flops 84213824 | bytes 4490093 | solution.py:68
  207.8 0.6 constant_dynamic-slice_fusion.8
  211.1 1.4 fusion.37
  212.5 0.6 constant_dynamic-slice_fusion.8
  215.8 1.4 fusion.37
  217.3 0.6 constant_dynamic-slice_fusion.8
  220.6 1.4 fusion.37
  222.1 0.6 constant_dynamic-slice_fusion.8
  225.4 1.4 fusion.37
  226.9 0.6 constant_dynamic-slice_fusion.8
  230.2 1.4 fusion.37
  231.6 0.6 constant_dynamic-slice_fusion.8
  234.9 1.4 fusion.37
  236.4 0.6 constant_dynamic-slice_fusion.8
  239.7 1.4 fusion.37
  241.2 0.6 constant_dynamic-slice_fusion.8
  244.5 1.4 fusion.37
  246.0 0.6 constant_dynamic-slice_fusion.8
  249.3 1.4 fusion.37
  250.7 0.6 constant_dynamic-slice_fusion.8
  254.0 1.4 fusion.37
  255.5 4.2 %pad_maximum_fusion = f32[4,512,512]{2,1,0:T(8,128)} fusion(f32[2,512,512]{2,1,0:T(8,128)} %get-tuple-element.300, f32[2,512,512]{2,1,0:T(8,128)S(1)} %get-tuple-element.299), kind=kLoop, calls=%fused_computation.23 | loop fusion | flops 1048576 | bytes 8388608 | tf_op jit(solution)/shard_map/concatenate | solution.py:70
  259.7 79.4 %reduce-scatter.2.cloned.1.call-done = f32[4,32,512]{2,1,0:T(8,128)} async-done(((f32[4,512,512]{2,1,0:T(8,128)}), f32[4,32,512]{2,1,0:T(8,128)}) %reduce-scatter.2.cloned.1.call-update) | async-done | bytes 262160 | tf_op jit(solution)/shard_map/reduce_scatter | solution.py:71
  (33 shorter events, 6.6 us)
Async XLA Ops:
  6.5 107.2 %copy-start = (bf16[2,18,128,128]{3,2,1,0:T(8,128)(2,1)S(1)}, bf16[2,18,128,128]{3,2,1,0:T(8,128)(2,1)}, u32[]{:S(2)}) copy-start(bf16[2,18,128,128]{3,2,1,0:T(8,128)(2,1)} %param.8) | copy-start | bytes 3538948
  6.5 107.1 %copy-start.1 = (s32[2,18]{1,0:T(2,128)S(1)}, s32[2,18]{1,0:T(2,128)}, u32[]{:S(2)}) copy-start(s32[2,18]{1,0:T(2,128)} %param.9) | copy-start | bytes 436
  6.5 47.2 %all-gather.3.cloned.1.call-start = ((), (), s32[]{:S(2)}) async-start(), calls=%async_computation.1 | async-start | bytes 2228224 | tf_op jit(solution)/shard_map/all_gather | solution.py:35
  7.3 108.1 %all-gather.5.cloned.1.call-start = ((), (), s32[]{:S(2)}) async-start(), calls=%async_computation.2 | async-start | bytes 6291456 | tf_op jit(solution)/shard_map/all_gather | solution.py:36
  53.7 285.4 %reduce-scatter.2.cloned.1.call-start = ((), (), s32[]{:S(2)}) async-start(), calls=%async_computation.3 | async-start | bytes 4456448 | tf_op jit(solution)/shard_map/reduce_scatter | solution.py:71
  53.8 59.9 %collective-permute-start.2 = (bf16[2,18,128,128]{3,2,1,0:T(8,128)(2,1)}, bf16[2,18,128,128]{3,2,1,0:T(8,128)(2,1)S(1)}, u32[]{:S(2)}, u32[]{:S(2)}) collective-permute-start(bf16[2,18,128,128]{3,2,1,0:T(8,128)(2,1)} %param.8), channel_id=1, source_target_pairs={{0,8},{1,9},{2,10},{3,11},{4,12},{5,13},{6,14},{7,15},{8,0},{9,1},... | collective-permute-start | bytes 3538952 | tf_op jit(solution)/shard_map/ppermute | solution.py:12
  54.5 53.8 %collective-permute-start = (s32[2,1]{0,1:T(1,128)}, s32[2,1]{0,1:T(1,128)S(1)}, u32[]{:S(2)}, u32[]{:S(2)}) collective-permute-start(s32[2,1]{0,1:T(1,128)} %param.10), channel_id=1, source_target_pairs={{0,8},{1,9},{2,10},{3,11},{4,12},{5,13},{6,14},{7,15},{8,0},{9,1},... | collective-permute-start | bytes 32 | tf_op jit(solution)/shard_map/ppermute | solution.py:12
  56.8 56.9 %collective-permute-start.1 = (s32[2,18]{1,0:T(2,128)}, s32[2,18]{1,0:T(2,128)S(1)}, u32[]{:S(2)}, u32[]{:S(2)}) collective-permute-start(s32[2,18]{1,0:T(2,128)} %param.9), channel_id=1, source_target_pairs={{0,8},{1,9},{2,10},{3,11},{4,12},{5,13},{6,14},{7,15},{8,0},{9,1},... | collective-permute-start | bytes 440 | tf_op jit(solution)/shard_map/ppermute | solution.py:12
Sparse Core Ops, SparseCore 0:
  9.5 44.1 all-gather.2
  55.2 55.3 all-gather.4
  259.8 79.2 reduce-scatter.1
where the time goes:
time: 348 us; the launch traced here: 346 us
  waiting for transfers between devices  176 us (51%)
  loops' own time  60.4 us (17%)
  matrix products  46.2 us (13%)
  local copies, waits for them, and re-layouts  35.5 us (10%)
  between operations  18 us (5%)
  other arithmetic  5.86 us (2%)
  starting transfers between devices  3.69 us (1%)
    reduce_scatter x1, waiting for transfers between devices, body(): return lax.psum_scatter(joined, 'pq', scatter_dimension=1, tiled=True)  79.4 us
    another operation x2, loops' own time, body(): totals = lax.fori_loop(lower_bound, upper_bound, step, empty)  60.4 us
    ppermute x3, waiting for transfers between devices, partner(): return lax.ppermute(value, axis, pairs)  49.5 us
    all_gather x1, waiting for transfers between devices, body(): coef_rows = lax.all_gather(coef, 'pq', axis=0, tiled=True)  46.4 us
    dot_general x23, matrix products, block_term(): lax.dot_general(row_coef, half, (((0,), (0,)), ((), ())), preferred_eleme...  46.2 us
    dynamic_slice x23, local copies, waits for them, and re-layouts, add_term(): current = lax.dynamic_index_in_dim(total, which, 0, keepdims=False)  17.6 us
    dynamic_slice x23, local copies, waits for them, and re-layouts, step(): ident = stacked_list[source, panel, place]  14 us
  transfers between devices with their start and end apart: 6, of which 3 were waited for; matrix products, arithmetic and copies ran while one was open for 1% of the time, Pallas kernels for 0%

commit v1 on v0

--- a/solution.py
+++ b/solution.py
@@ -33,7 +33,11 @@
 
 def body(pair_blocks, block_list, block_count, coef):
     coef_rows = lax.all_gather(coef, "pq", axis=0, tiled=True)
-    coef_full = lax.all_gather(coef_rows, "grp", axis=1, tiled=True)
+    coef_full = jnp.roll(
+        jnp.concatenate([coef_rows, lax.ppermute(coef_rows, "grp", [(0, 1), (1, 0)])], axis=1),
+        lax.axis_index("grp") * coef_rows.shape[1],
+        axis=1,
+    )
     panels = pair_blocks.shape[0]
     tile = pair_blocks.shape[2]
     nblk = coef_full.shape[0] // tile

time: 348 us -> 367 us (1.055)
  waiting for transfers between devices: 176 us -> 194 us
  other arithmetic: 5.86 us -> 11.8 us
    reduce_scatter x1, waiting for transfers between devices: 79.4 us -> 97.8 us  [body(): return lax.psum_scatter(joined, 'pq', scatter_dimension=1, tiled=True)]
    concatenate x0 -> x1, other arithmetic: none -> 4.1 us  [body(): jnp.roll(jnp.concatenate([coef_rows, lax.ppermute(coef_rows, 'grp', [(0,...]
  transfers between devices with their start and end apart: 6 -> 6, of which waited for: 3 -> 3; matrix products, arithmetic and copies ran while one was open for 1% -> 2% of each run, Pallas kernels for 0% -> 0%
where the time goes in v1:
time: 367 us; the launch traced here: 365 us
  waiting for transfers between devices  194 us (53%)
  loops' own time  60.4 us (16%)
  matrix products  43.3 us (12%)
  local copies, waits for them, and re-layouts  32.1 us (9%)
  between operations  18.3 us (5%)
  other arithmetic  11.8 us (3%)
  starting transfers between devices  5.05 us (1%)
    reduce_scatter x1, waiting for transfers between devices, body(): return lax.psum_scatter(joined, 'pq', scatter_dimension=1, tiled=True)  97.8 us
    another operation x2, loops' own time, body(): totals = lax.fori_loop(lower_bound, upper_bound, step, empty)  60.4 us
    ppermute x3, waiting for transfers between devices, partner(): return lax.ppermute(value, axis, pairs)  49.3 us
    all_gather x1, waiting for transfers between devices, body(): coef_rows = lax.all_gather(coef, 'pq', axis=0, tiled=True)  46.4 us
    dot_general x23, matrix products, block_term(): lax.dot_general(row_coef, half, (((0,), (0,)), ((), ())), preferred_eleme...  43.3 us
    dynamic_slice x23, local copies, waits for them, and re-layouts, step(): ident = stacked_list[source, panel, place]  14.3 us
    dynamic_slice x23, local copies, waits for them, and re-layouts, add_term(): current = lax.dynamic_index_in_dim(total, which, 0, keepdims=False)  14 us
  transfers between devices with their start and end apart: 6, of which 3 were waited for; matrix products, arithmetic and copies ran while one was open for 2% of the time, Pallas kernels for 0%

profile of v1, /device:TPU:0, one launch (start us, length us, event | category | flops | bytes accessed | tf_op | source)
XLA Modules:
  0.0 365.2 jit_solution(14472214944982338774)
XLA Ops:
  6.5 0.7 all-gather.2.cloned.1.call-update
  7.3 46.4 %all-gather.2.cloned.1.call-done = bf16[4096,256]{1,0:T(8,128)(2,1)} async-done(((bf16[256,256]{1,0:T(8,128)(2,1)}), bf16[4096,256]{1,0:T(8,128)(2,1)}) %all-gather.2.cloned.1.call-update) | async-done | bytes 2097168 | tf_op jit(solution)/shard_map/all_gather | solution.py:35
  53.7 1.5 collective-permute-start.2
  55.2 0.6 collective-permute-start.3
  55.8 2.3 collective-permute-start
  58.1 0.6 collective-permute-start.1
  58.7 1.3 fusion.28
  60.0 49.3 %collective-permute-done = s32[2,1]{0,1:T(1,128)S(1)} collective-permute-done((s32[2,1]{0,1:T(1,128)}, s32[2,1]{0,1:T(1,128)S(1)}, u32[]{:S(2)}, u32[]{:S(2)}) %collective-permute-start) | collective-permute-done | bytes 40 | tf_op jit(solution)/shard_map/ppermute | solution.py:12
  109.3 0.6 fusion.27
  114.8 0.7 pad_add_fusion
  115.5 3.1 pad_maximum_fusion.1
  118.6 4.1 %fusion.26 = bf16[4096,512]{1,0:T(8,128)(2,1)} fusion(s32[]{:T(128)S(6)} %select_n.229, bf16[4096,256]{1,0:T(8,128)(2,1)S(1)} %copy-done, bf16[4096,256]{1,0:T(8,128)(2,1)S(1)} %collective-permute-done.2), kind=kLoop, calls=%fused_computation.29 | loop fusion | flops 16777216 | bytes 8388612 | tf_op jit(solution)/shard_map/jit(_roll_dynamic)/concatenate | solution.py:36
  122.7 1.7 broadcast_in_dim.18.clone.1
  124.3 69.7 %while.26 = (s32[]{:T(128)}, f32[2,512,512]{2,1,0:T(8,128)}, s32[]{:T(128)}, s32[]{:T(128)}, s32[]{:T(128)}, /*index=5*/s32[]{:T(128)}, s32[2,2,18]{2,1,0:T(2,12...) while((s32[]{:T(128)}, f32[2,512,512]{2,1,0:T(8,128)}, ...), condition=%wide.region_1.2_spmd, body=%wide.region_0.1_spmd.sunk | while | flops 84213824 | bytes 4490085 | solution.py:72
  124.3 0.6 constant_dynamic-slice_fusion.8
  127.5 1.3 constant_dynamic-slice_fusion.9
  128.8 2.5 fusion.40
  134.6 1.3 constant_dynamic-slice_fusion.9
  135.9 2.4 fusion.40
  141.5 1.3 constant_dynamic-slice_fusion.9
  142.8 2.5 fusion.40
  148.5 1.3 constant_dynamic-slice_fusion.9
  149.8 2.4 fusion.40
  155.4 1.3 constant_dynamic-slice_fusion.9
  156.7 2.5 fusion.40
  162.5 1.3 constant_dynamic-slice_fusion.9
  163.8 2.5 fusion.40
  169.5 1.3 constant_dynamic-slice_fusion.9
  170.8 2.4 fusion.40
  176.4 1.3 constant_dynamic-slice_fusion.9
  177.7 2.4 fusion.40
  183.3 1.3 constant_dynamic-slice_fusion.9
  184.6 2.4 fusion.40
  190.2 1.3 constant_dynamic-slice_fusion.9
  191.5 2.5 fusion.40
  194.3 62.3 %while.27 = (s32[]{:T(128)}, f32[2,512,512]{2,1,0:T(8,128)S(1)}, s32[]{:T(128)}, s32[]{:T(128)}, s32[]{:T(128)}, /*index=5*/s32[]{:T(128)}, s32[2,2,18]{2,1,0:T(...) while((s32[]{:T(128)}, f32[2,512,512]{2,1,0:T(8,128)S(1)}, ...), condition=%wide.region_3.4_spmd, body=%wide.region_2.3_spmd.sunk | while | flops 84213824 | bytes 4490085 | solution.py:72
  194.4 0.6 constant_dynamic-slice_fusion.10
  197.7 1.4 fusion.44
  199.2 0.6 constant_dynamic-slice_fusion.10
  202.5 1.4 fusion.44
  203.9 0.6 constant_dynamic-slice_fusion.10
  207.2 1.4 fusion.44
  208.7 0.6 constant_dynamic-slice_fusion.10
  212.0 1.4 fusion.44
  213.5 0.6 constant_dynamic-slice_fusion.10
  216.8 1.4 fusion.44
  218.3 0.6 constant_dynamic-slice_fusion.10
  221.6 1.4 fusion.44
  223.1 0.6 constant_dynamic-slice_fusion.10
  226.4 1.4 fusion.44
  227.9 0.6 constant_dynamic-slice_fusion.10
  231.2 1.4 fusion.44
  232.7 0.6 constant_dynamic-slice_fusion.10
  236.0 1.4 fusion.44
  237.5 0.6 constant_dynamic-slice_fusion.10
  240.8 1.4 fusion.44
  242.3 0.6 constant_dynamic-slice_fusion.10
  245.6 1.4 fusion.44
  247.0 0.6 constant_dynamic-slice_fusion.10
  250.3 1.4 fusion.44
  251.8 0.6 constant_dynamic-slice_fusion.10
  255.1 1.4 fusion.44
  256.6 4.0 %pad_maximum_fusion = f32[4,512,512]{2,1,0:T(8,128)} fusion(f32[2,512,512]{2,1,0:T(8,128)S(1)} %get-tuple-element.300, f32[2,512,512]{2,1,0:T(8,128)} %get-tuple-element.299), kind=kLoop, calls=%fused_computation.30 | loop fusion | flops 1048576 | bytes 8388608 | tf_op jit(solution)/shard_map/concatenate | solution.py:74
  260.6 97.8 %reduce-scatter.2.cloned.1.call-done = f32[4,32,512]{2,1,0:T(8,128)} async-done(((f32[4,512,512]{2,1,0:T(8,128)}), f32[4,32,512]{2,1,0:T(8,128)}) %reduce-scatter.2.cloned.1.call-update) | async-done | bytes 262160 | tf_op jit(solution)/shard_map/reduce_scatter | solution.py:75
  (31 shorter events, 6.7 us)
Async XLA Ops:
  6.5 47.2 %all-gather.2.cloned.1.call-start = ((), (), s32[]{:S(2)}) async-start(), calls=%async_computation.1 | async-start | bytes 2228224 | tf_op jit(solution)/shard_map/all_gather | solution.py:35
  7.3 351.1 %reduce-scatter.2.cloned.1.call-start = ((), (), s32[]{:S(2)}) async-start(), calls=%async_computation.2 | async-start | bytes 4456448 | tf_op jit(solution)/shard_map/reduce_scatter | solution.py:75
  53.7 64.9 %collective-permute-start.2 = (bf16[4096,256]{1,0:T(8,128)(2,1)}, bf16[4096,256]{1,0:T(8,128)(2,1)S(1)}, u32[]{:S(2)}, u32[]{:S(2)}) collective-permute-start(bf16[4096,256]{1,0:T(8,128)(2,1)} %all-gather.2.cloned.1.call-done), channel_id=1, source_target_pairs={{0,16},{16,0},{1,17},{17,1},{2,18},{18,2},{3,19},{19,3},{4,20},{20... | collective-permute-start | bytes 6291464 | tf_op jit(solution)/shard_map/ppermute | solution.py:37
  55.2 60.3 %collective-permute-start.3 = (bf16[2,18,128,128]{3,2,1,0:T(8,128)(2,1)}, bf16[2,18,128,128]{3,2,1,0:T(8,128)(2,1)S(1)}, u32[]{:S(2)}, u32[]{:S(2)}) collective-permute-start(bf16[2,18,128,128]{3,2,1,0:T(8,128)(2,1)} %param.8), channel_id=1, source_target_pairs={{0,8},{1,9},{2,10},{3,11},{4,12},{5,13},{6,14},{7,15},{8,0},{9,1},... | collective-permute-start | bytes 3538952 | tf_op jit(solution)/shard_map/ppermute | solution.py:12
  55.8 53.5 %collective-permute-start = (s32[2,1]{0,1:T(1,128)}, s32[2,1]{0,1:T(1,128)S(1)}, u32[]{:S(2)}, u32[]{:S(2)}) collective-permute-start(s32[2,1]{0,1:T(1,128)} %param.10), channel_id=1, source_target_pairs={{0,8},{1,9},{2,10},{3,11},{4,12},{5,13},{6,14},{7,15},{8,0},{9,1},... | collective-permute-start | bytes 32 | tf_op jit(solution)/shard_map/ppermute | solution.py:12
  58.1 56.7 %collective-permute-start.1 = (s32[2,18]{1,0:T(2,128)}, s32[2,18]{1,0:T(2,128)S(1)}, u32[]{:S(2)}, u32[]{:S(2)}) collective-permute-start(s32[2,18]{1,0:T(2,128)} %param.9), channel_id=1, source_target_pairs={{0,8},{1,9},{2,10},{3,11},{4,12},{5,13},{6,14},{7,15},{8,0},{9,1},... | collective-permute-start | bytes 440 | tf_op jit(solution)/shard_map/ppermute | solution.py:12
  115.5 3.1 copy-start
Sparse Core Ops, SparseCore 0:
  9.5 44.1 all-gather.1
  260.7 97.6 reduce-scatter.1
